TPU v7x, 32 devices: a whole 2x2x4 slice. The times are simulated.
32 devices in a mesh: ell: 4 (over y, x), blk: 8 (over z, core).
Axes of the slice: x: 2, y: 2, z: 4, core: 2. Of those that a mesh axis runs over, the one named last changes fastest.
Arguments:
- wigner: bfloat16 [8, 17, 2101248], P(None, None, ('ell', 'blk')), may hold values from -6 to 6
- sky_alm: float32 [2, 2101248], P(None, ('ell', 'blk')), may hold values from -0.03125 to 0.03125
- beam_blm: float32 [2, 17, 2048], replicated, may hold values from -4.25 to 4.25
- slot_col: int32 [2101248], P(('ell', 'blk')), may hold values from -1 to 255, as said below
- slot_ell: int32 [2101248], P(('ell', 'blk')), may hold values from 0 to 2047, as said below
- order_of_column: int32 [2048], replicated, may hold values from 0 to 2047, as said below
Outputs:
- conv_cube: float32 [8, 32, 4096], P('ell', 'blk')
Inputs may be any that keep to these rules, and one draw needn't show every extreme that they name: `slot_col`: slot block b (slots b * 65664 to b * 65664 + 65663) belongs to ell index b // 8 and blk index b % 8; at most 65568 slots of a block are live, and some blocks have exactly that many. `slot_ell`: every pair (l, m) with m <= l < 2048 stands in exactly one live slot; within a blk group, higher ell indices hold degrees no lower than those of lower ell indices. `order_of_column`: A permutation of 0 to 2047; every blk group's orders hold the same number of pairs.
All inputs are finite; a program needn't handle non-finite values.
Results may differ from a plain program's by a relative error of at most 0.0029.
Values sent between devices are 32-bit elements; how exact they have to be, the bound alone decides.
A program may use at most 256 MiB of HBM per device.

v0:
```python
import math

import jax
import jax.numpy as jnp
from jax import lax
from jax.sharding import PartitionSpec as P

NPSI = 32


def phase_table(rows, cols, period):
    product = (
        jnp.arange(rows, dtype=jnp.int32)[:, None]
        * jnp.arange(cols, dtype=jnp.int32)[None, :]
        % period
    )
    angle = product.astype(jnp.float32) * (2.0 * math.pi / period)
    return (jnp.cos(angle), jnp.sin(angle))


def psi_table(order_count, samples):
    cosines, sine_terms = phase_table(order_count, samples, samples)
    real_row = jnp.stack([cosines, sine_terms], axis=1)
    imag_row = jnp.stack([-sine_terms, cosines], axis=1)
    return jnp.stack([real_row, imag_row], axis=0)


def to_psi(harmonic, table):
    return jnp.einsum("trkc,rksp->tspc", harmonic, table, precision=lax.Precision.HIGHEST)


def to_phi(fields, order_of_column):
    cycles = fields.shape[0]
    samples = fields.shape[2]
    degrees = fields.shape[3]
    period = 2 * degrees
    inner = 2 ** ((period.bit_length() - 1) // 2)
    outer = period // inner
    highest = lax.Precision.HIGHEST
    high_part = order_of_column // inner
    low_part = order_of_column % inner
    turns = high_part[:, None] * jnp.arange(outer, dtype=jnp.int32)[None, :] % outer
    angle = turns.astype(jnp.float32) * (2.0 * math.pi / outer)
    cos_first = jnp.cos(angle)
    sin_first = jnp.sin(angle)
    select = (low_part[:, None] == jnp.arange(inner, dtype=jnp.int32)[None, :]).astype(jnp.float32)
    real_in = fields[:, 0]
    imag_in = fields[:, 1]
    weighted_re = real_in[..., None] * cos_first - imag_in[..., None] * sin_first
    weighted_im = real_in[..., None] * sin_first + imag_in[..., None] * cos_first
    first_re = jnp.einsum("tpcj,cv->tpvj", weighted_re, select, precision=highest)
    first_im = jnp.einsum("tpcj,cv->tpvj", weighted_im, select, precision=highest)
    cos_twist, sin_twist = phase_table(inner, outer, period)
    twist_re = first_re * cos_twist - first_im * sin_twist
    twist_im = first_re * sin_twist + first_im * cos_twist
    cos_last, sin_last = phase_table(inner, inner, inner)
    result = jnp.einsum("tpvj,vw->tpwj", twist_re, cos_last, precision=highest) - jnp.einsum(
        "tpvj,vw->tpwj", twist_im, sin_last, precision=highest
    )
    return result.reshape(cycles, samples, period)


def on_device(wigner, sky_alm, beam_blm, slot_col, slot_ell, order_of_column):
    cycle_total = wigner.shape[0]
    order_count = wigner.shape[1]
    slot_count = wigner.shape[2]
    ell_count = lax.axis_size("ell")
    blk_count = lax.axis_size("blk")
    col_count = order_of_column.shape[0] // blk_count
    cycle_share = cycle_total // ell_count
    degree_count = beam_blm.shape[2]
    beam_rows = beam_blm.reshape(2 * order_count, degree_count).T
    picked = jnp.take(beam_rows, slot_ell, axis=0)
    beam_slots = picked.T.reshape(2, order_count, slot_count)
    coeffs = jnp.stack(
        [
            sky_alm[0] * beam_slots[0] - sky_alm[1] * beam_slots[1],
            sky_alm[0] * beam_slots[1] + sky_alm[1] * beam_slots[0],
        ]
    )
    one_hot = (slot_col[:, None] == jnp.arange(col_count, dtype=jnp.int32)[None, :]).astype(
        jnp.bfloat16
    )
    table = psi_table(order_count, NPSI)
    values = (wigner[:, None].astype(jnp.float32) * coeffs[None]).astype(jnp.bfloat16)
    col_sums = jnp.dot(values.reshape(-1, slot_count), one_hot, preferred_element_type=jnp.float32)
    summed = lax.psum_scatter(
        col_sums.reshape(cycle_share * lax.axis_size("ell"), 2, order_count, col_count),
        "ell",
        scatter_dimension=0,
        tiled=True,
    )
    owned = to_psi(summed, table)
    return to_phi(
        lax.all_to_all(owned, "blk", split_axis=2, concat_axis=3, tiled=True), order_of_column
    )


def solution(mesh):
    return jax.shard_map(
        on_device,
        mesh=mesh,
        in_specs=(
            P(None, None, ("ell", "blk")),
            P(None, ("ell", "blk")),
            P(),
            P(("ell", "blk")),
            P(("ell", "blk")),
            P(),
        ),
        out_specs=P("ell", "blk", None),
        check_vma=False,
    )
```

profile of v0, /device:TPU:0, one launch (start us, length us, event | category | flops | bytes accessed | tf_op | source)
XLA Modules:
  0.0 433.9 jit_solution(10651891721096126606)
XLA Ops:
  6.5 1.0 compare_select_fusion
  7.5 1.0 compare_and_fusion
  8.6 2.7 slice_reduce_fusion.1
  11.2 1.1 copy.43
  12.4 0.4 copy.44
  12.8 120.9 %gather_fusion = f32[65664,34]{1,0:T(8,128)} fusion(f32[2048,34]{1,0:T(8,128)S(1)} %bitcast.72, s32[66560]{0:T(1024)S(1)} %pad_clamp_fusion), kind=kCustom, calls=%fused_computation | custom fusion | bytes 18123264 | tf_op jit(solution)/shard_map/jit(_take)/gather | solution.py:73
  133.7 36.4 %select_bitcast_fusion = f32[34,65664]{0,1:T(8,128)} fusion(f32[65664,34]{1,0:T(8,128)} %gather_fusion, pred[65664]{0:T(1024)(128)(4,1)S(1)} %compare_and_fusion), kind=kLoop, calls=%fused_computation.11 | loop fusion | flops 2232576 | bytes 17926272 | tf_op jit(solution)/shard_map/jit(_take)/select_n | solution.py:73
  170.1 45.0 %subtract_bitcast_fusion = (f32[1,17,65664]{1,2,0:T(8,128)}, f32[1,17,65664]{1,2,0:T(8,128)}) fusion(f32[34,65664]{0,1:T(8,128)} %select_bitcast_fusion, f32[65664]{0:T(1024)S(1)} %get-tuple-element.6, f32[65664]{0:T(1024)S(1)} %get-tuple-element.5), kind=kLoop, calls=%fused_computation.10 | loop fusion | flops 6697728 | bytes 18385920 | tf_op jit(solution)/shard_map/stack | solution.py:75
  215.1 44.3 %pad_maximum_fusion = f32[2,17,65664]{1,2,0:T(8,128)} fusion(f32[1,17,65664]{1,2,0:T(8,128)} %get-tuple-element.8, f32[1,17,65664]{1,2,0:T(8,128)} %get-tuple-element.7), kind=kLoop, calls=%fused_computation.2 | loop fusion | flops 2232576 | bytes 17860608 | tf_op jit(solution)/shard_map/stack | solution.py:75
  259.4 38.5 %copy.45 = f32[2,17,65664]{2,1,0:T(8,128)} copy(f32[2,17,65664]{1,2,0:T(8,128)} %pad_maximum_fusion) | data formatting | bytes 17860608 | tf_op jit(solution)/shard_map/stack | solution.py:75
  297.8 22.0 %copy.42 = f32[8,17,65664]{2,1,0:T(8,128)} copy(bf16[8,17,65664]{2,0,1:T(8,128)(2,1)} %param.6) | data formatting | bytes 53581824 | tf_op jit(solution)/shard_map/convert_element_type | solution.py:85
  319.9 30.2 %fusion.94 = pred[65664,256,1,1]{1,0,3,2:T(32,128)(4,1)S(1)} fusion(s32[65664]{0:T(1024)S(1)} %copy-done), kind=kLoop, calls=%fused_computation.4.clone.clone.2 | loop fusion | flops 16809984 | bytes 17072640 | tf_op jit(solution)/shard_map/dot_general | solution.py:86
  350.1 27.0 %fusion.1 = f32[8,2,17,256]{3,2,1,0:T(8,128)} fusion(f32[2,17,65664]{2,1,0:T(8,128)} %copy.45, f32[8,17,65664]{2,1,0:T(8,128)} %copy.42, pred[65664,256,1,1]{1,0,3,2:T(32,128)(4,1)S(1)} %fusion.94), kind=kOutput, calls=%fused_computation.5 | convolution fusion | flops 9180352512 | bytes 61740032 | tf_op jit(solution)/shard_map/dot_general | solution.py:86
  377.3 27.4 %reduce-scatter.2.cloned.1.call-done = f32[2,2,17,256]{3,2,1,0:T(8,128)} async-done(((f32[8,2,17,256]{3,2,1,0:T(8,128)}), f32[2,2,17,256]{3,2,1,0:T(8,128)}) %reduce-scatter.2.cloned.1.call-update) | async-done | bytes 69648 | tf_op jit(solution)/shard_map/reduce_scatter | solution.py:87
  404.7 1.2 convolution_bitcast_fusion
  405.9 0.8 copy.46
  406.7 4.6 %all-to-all-start = ((f32[2,2,32,256]{3,0,1,2:T(2,128)}), f32[2,2,32,256]{3,0,1,2:T(2,128)S(1)}, u32[]{:S(2)}, u32[]{:S(2)}) async-start(f32[2,2,32,256]{3,0,1,2:T(2,128)} %copy.46), calls=%async_computation.1 | async-start | bytes 262144 | tf_op jit(solution)/shard_map/all_to_all | solution.py:95
  411.2 2.0 fusion.42
  413.7 4.3 all-to-all-done
  418.2 3.5 fusion.10
  421.6 3.5 fusion.6
  425.1 0.5 fusion.33
  425.7 0.5 fusion.22
  426.2 0.8 reshape.187
  (19 shorter events, 0.9 us)
Async XLA Ops:
  6.5 398.1 %reduce-scatter.2.cloned.1.call-start = ((), (), s32[]{:S(2)}) async-start(), calls=%async_computation.2 | async-start | bytes 491520 | tf_op jit(solution)/shard_map/reduce_scatter | solution.py:87
  297.8 22.0 %copy-start = (s32[65664]{0:T(1024)S(1)}, s32[65664]{0:T(1024)}, u32[]{:S(2)}) copy-start(s32[65664]{0:T(1024)} %param.9) | copy-start | bytes 787972
  350.1 27.2 %copy-start.1 = (s32[2048]{0:T(1024)S(1)}, s32[2048]{0:T(1024)}, u32[]{:S(2)}) copy-start(s32[2048]{0:T(1024)} %param.11) | copy-start | bytes 24580
  406.7 11.3 %all-to-all-start = ((f32[2,2,32,256]{3,0,1,2:T(2,128)}), f32[2,2,32,256]{3,0,1,2:T(2,128)S(1)}, u32[]{:S(2)}, u32[]{:S(2)}) async-start(f32[2,2,32,256]{3,0,1,2:T(2,128)} %copy.46), calls=%async_computation.1 | async-start | bytes 262144 | tf_op jit(solution)/shard_map/all_to_all | solution.py:95
Sparse Core Ops, SparseCore 0:
  377.2 27.4 reduce-scatter.1
where the time goes:
time: 435 us; the launch traced here: 434 us
  local copies, waits for them, and re-layouts  187 us (43%)
  other arithmetic  160 us (37%)
  matrix products  36.2 us (8%)
  waiting for transfers between devices  31.7 us (7%)
  between operations  13.5 us (3%)
  starting transfers between devices  4.59 us (1%)
    gather x1, local copies, waits for them, and re-layouts, on_device(): picked = jnp.take(beam_rows, slot_ell, axis=0)  121 us
    another operation x2, other arithmetic, on_device(): jnp.stack([sky_alm[0] * beam_slots[0] - sky_alm[1] * beam_slots[1], sky_a...  89.3 us
    another operation x1, local copies, waits for them, and re-layouts, on_device(): jnp.stack([sky_alm[0] * beam_slots[0] - sky_alm[1] * beam_slots[1], sky_a...  38.5 us
    select_n x2, other arithmetic, on_device(): picked = jnp.take(beam_rows, slot_ell, axis=0)  37.4 us
    dot_general x1, other arithmetic, on_device(): jnp.dot(values.reshape(-1, slot_count), one_hot, preferred_element_type=j...  30.2 us
    reduce_scatter x1, waiting for transfers between devices, on_device(): lax.psum_scatter(col_sums.reshape(cycle_share * lax.axis_size('ell'), 2,...  27.4 us
    dot_general x1, matrix products, on_device(): jnp.dot(values.reshape(-1, slot_count), one_hot, preferred_element_type=j...  27 us
    convert_element_type x1, local copies, waits for them, and re-layouts, on_device(): wigner[:, None].astype(jnp.float32) * coeffs[None]  22 us
  transfers between devices with their start and end apart: 2, of which 2 were waited for; matrix products, arithmetic and copies ran while one was open for 1% of the time, Pallas kernels for 0%

commit v1 on v0

--- a/solution.py
+++ b/solution.py
@@ -1,11 +1,16 @@
+import functools
 import math
 
 import jax
 import jax.numpy as jnp
 from jax import lax
+from jax.experimental import pallas as pl
+from jax.experimental.pallas import tpu as pltpu
 from jax.sharding import PartitionSpec as P
 
 NPSI = 32
+LANES = 128
+SUBLANES = 8
 
 
 def phase_table(rows, cols, period):
@@ -23,10 +28,6 @@
     real_row = jnp.stack([cosines, sine_terms], axis=1)
     imag_row = jnp.stack([-sine_terms, cosines], axis=1)
     return jnp.stack([real_row, imag_row], axis=0)
-
-
-def to_psi(harmonic, table):
-    return jnp.einsum("trkc,rksp->tspc", harmonic, table, precision=lax.Precision.HIGHEST)
 
 
 def to_phi(fields, order_of_column):
@@ -60,37 +61,190 @@
     return result.reshape(cycles, samples, period)
 
 
+def largest_part(total, most):
+    return max(part for part in range(1, total + 1) if total % part == 0 and part <= most)
+
+
+def beam_table(beam):
+    orders, degrees = beam.shape[1], beam.shape[2]
+    whole = orders // SUBLANES * SUBLANES
+    rest = orders - whole
+    rows = [beam[0, :whole], beam[1, :whole]]
+    if rest > 0:
+        real, imag = beam[0, whole:], beam[1, whole:]
+        short = SUBLANES // 4 if rest <= SUBLANES // 4 else SUBLANES
+        real = jnp.pad(real, ((0, short - rest), (0, 0)))
+        imag = jnp.pad(imag, ((0, short - rest), (0, 0)))
+        rows += [real, imag, -imag, real] if short < SUBLANES else [real, imag]
+    table = jnp.concatenate(rows, axis=0)
+    tiles = degrees // LANES
+    return table.reshape(table.shape[0], tiles, LANES).transpose(1, 0, 2)
+
+
+def lane_pick(table, index):
+    return lax.gather(
+        table,
+        index[..., None],
+        lax.GatherDimensionNumbers(
+            offset_dims=(),
+            collapsed_slice_dims=(1,),
+            start_index_map=(1,),
+            operand_batching_dims=(0,),
+            start_indices_batching_dims=(0,),
+        ),
+        slice_sizes=(1, 1),
+        mode=lax.GatherScatterMode.PROMISE_IN_BOUNDS,
+    )
+
+
+def sums_kernel(
+    orders, sub, wig_ref, sky_ref, col_ref, ell_ref, table_ref, out_ref, coeff_ref, value_ref, hot_ref
+):
+    cycles = wig_ref.shape[1]
+    chunk = wig_ref.shape[2]
+    tiles, rows, _ = table_ref.shape
+    groups = rows // SUBLANES
+    whole = orders // SUBLANES
+    rest = orders - whole * SUBLANES
+    packed = 0 < rest <= SUBLANES // 4
+    cols = hot_ref.shape[0]
+    parts = sub // LANES
+
+    live = col_ref[...] >= 0
+    degree = ell_ref[...]
+    top = jnp.max(jnp.where(live, degree, 0).astype(jnp.float32)).astype(jnp.int32) // LANES
+    low = jnp.min(jnp.where(live, degree, tiles * LANES - 1).astype(jnp.float32)).astype(jnp.int32) // LANES
+    span = top - low + 1
+
+    def pick_all(count, first, start):
+        for part in range(parts):
+            lanes = pl.ds(pl.multiple_of(start + part * LANES, LANES), LANES)
+            ell = jnp.broadcast_to(ell_ref[:, lanes], (SUBLANES, LANES))
+            high = (ell >> 7) - first
+            index = ell & (LANES - 1)
+            picked = [jnp.zeros((SUBLANES, LANES), jnp.float32) for _ in range(groups)]
+            for tile in range(count):
+                here = high == tile
+                for group in range(groups):
+                    entry = table_ref[first + tile, pl.ds(group * SUBLANES, SUBLANES), :]
+                    picked[group] = jnp.where(here, lane_pick(entry, index), picked[group])
+            sky_re = jnp.broadcast_to(sky_ref[0:1, lanes], (SUBLANES, LANES))
+            sky_im = jnp.broadcast_to(sky_ref[1:2, lanes], (SUBLANES, LANES))
+            out = []
+            for group in range(whole):
+                out.append(sky_re * picked[group] - sky_im * picked[whole + group])
+            for group in range(whole):
+                out.append(sky_re * picked[whole + group] + sky_im * picked[group])
+            if packed:
+                row = lax.broadcasted_iota(jnp.int32, (SUBLANES, LANES), 0)
+                term = picked[2 * whole] * jnp.where(row < SUBLANES // 2, sky_re, sky_im)
+                out.append(term + pltpu.roll(term, SUBLANES // 2, 0))
+            elif rest > 0:
+                out.append(sky_re * picked[2 * whole] - sky_im * picked[2 * whole + 1])
+                out.append(sky_re * picked[2 * whole + 1] + sky_im * picked[2 * whole])
+            here = slice(part * LANES, (part + 1) * LANES)
+            for group, block in enumerate(out):
+                coeff_ref[pl.ds(group * SUBLANES, SUBLANES), here] = block
+
+    def row_of(part, order):
+        if order < whole * SUBLANES:
+            return part * whole * SUBLANES + order
+        step = SUBLANES // 4 if packed else SUBLANES
+        return 2 * whole * SUBLANES + part * step + order - whole * SUBLANES
+
+    def run(count, first):
+        @pl.loop(0, chunk // sub)
+        def _(step):
+            start = pl.multiple_of(step * sub, LANES)
+            pick_all(count, first, start)
+            lanes = pl.ds(start, sub)
+            for order in range(orders):
+                wig = wig_ref[order, :, lanes].astype(jnp.float32)
+                real = wig * coeff_ref[pl.ds(row_of(0, order), 1), :]
+                imag = wig * coeff_ref[pl.ds(row_of(1, order), 1), :]
+                both = jnp.concatenate([real, imag], axis=0).astype(jnp.bfloat16)
+                value_ref[pl.ds(order * 2 * cycles, 2 * cycles), lanes] = both
+            col = jnp.broadcast_to(col_ref[:, lanes], (cols, sub))
+            row = lax.broadcasted_iota(jnp.int32, (cols, sub), 0)
+            hot_ref[:, lanes] = (row == col).astype(jnp.float32).astype(jnp.bfloat16)
+
+    counts = sorted({min(c, tiles) for c in (4, 5, 9)})
+    below = 0
+    for count in counts:
+        first = jnp.minimum(low, tiles - count)
+
+        @pl.when((span > below) & (span <= count) if below else span <= count)
+        def _():
+            run(count, first)
+
+        below = count
+    if below < tiles:
+
+        @pl.when(span > below)
+        def _():
+            run(tiles, 0)
+
+    part = lax.dot_general(
+        value_ref[...],
+        hot_ref[...],
+        (((1,), (1,)), ((), ())),
+        preferred_element_type=jnp.float32,
+    )
+
+    @pl.when(pl.program_id(0) == 0)
+    def _():
+        out_ref[...] = part
+
+    @pl.when(pl.program_id(0) > 0)
+    def _():
+        out_ref[...] += part
+
+
+def order_sums(wigner, sky_alm, beam_blm, slot_col, slot_ell, cols):
+    cycles, orders, slots = wigner.shape
+    tiles = slots // LANES
+    chunk = LANES * largest_part(tiles, 64)
+    sub = LANES * largest_part(chunk // LANES, 3)
+    table = beam_table(beam_blm)
+    rows = orders * 2 * cycles
+    return pl.pallas_call(
+        functools.partial(sums_kernel, orders, sub),
+        out_shape=jax.ShapeDtypeStruct((rows, cols), jnp.float32),
+        grid=(slots // chunk,),
+        in_specs=[
+            pl.BlockSpec((orders, cycles, chunk), lambda i: (0, 0, i)),
+            pl.BlockSpec((2, chunk), lambda i: (0, i)),
+            pl.BlockSpec((1, chunk), lambda i: (0, i)),
+            pl.BlockSpec((1, chunk), lambda i: (0, i)),
+            pl.BlockSpec(table.shape, lambda i: (0, 0, 0)),
+        ],
+        out_specs=pl.BlockSpec((rows, cols), lambda i: (0, 0)),
+        scratch_shapes=[
+            pltpu.VMEM((table.shape[1], sub), jnp.float32),
+            pltpu.VMEM((rows, chunk), jnp.bfloat16),
+            pltpu.VMEM((cols, chunk), jnp.bfloat16),
+        ],
+        compiler_params=pltpu.CompilerParams(
+            dimension_semantics=("arbitrary",), vmem_limit_bytes=48 * 1024 * 1024
+        ),
+        name="order_sums",
+    )(wigner.transpose(1, 0, 2), sky_alm, slot_col[None, :], slot_ell[None, :], table)
+
+
 def on_device(wigner, sky_alm, beam_blm, slot_col, slot_ell, order_of_column):
     cycle_total = wigner.shape[0]
     order_count = wigner.shape[1]
-    slot_count = wigner.shape[2]
-    ell_count = lax.axis_size("ell")
     blk_count = lax.axis_size("blk")
     col_count = order_of_column.shape[0] // blk_count
-    cycle_share = cycle_total // ell_count
-    degree_count = beam_blm.shape[2]
-    beam_rows = beam_blm.reshape(2 * order_count, degree_count).T
-    picked = jnp.take(beam_rows, slot_ell, axis=0)
-    beam_slots = picked.T.reshape(2, order_count, slot_count)
-    coeffs = jnp.stack(
-        [
-            sky_alm[0] * beam_slots[0] - sky_alm[1] * beam_slots[1],
-            sky_alm[0] * beam_slots[1] + sky_alm[1] * beam_slots[0],
-        ]
-    )
-    one_hot = (slot_col[:, None] == jnp.arange(col_count, dtype=jnp.int32)[None, :]).astype(
-        jnp.bfloat16
-    )
-    table = psi_table(order_count, NPSI)
-    values = (wigner[:, None].astype(jnp.float32) * coeffs[None]).astype(jnp.bfloat16)
-    col_sums = jnp.dot(values.reshape(-1, slot_count), one_hot, preferred_element_type=jnp.float32)
-    summed = lax.psum_scatter(
-        col_sums.reshape(cycle_share * lax.axis_size("ell"), 2, order_count, col_count),
-        "ell",
-        scatter_dimension=0,
-        tiled=True,
-    )
-    owned = to_psi(summed, table)
+    col_sums = order_sums(wigner, sky_alm, beam_blm, slot_col, slot_ell, col_count)
+    by_cycle = col_sums.reshape(order_count, 2, cycle_total, col_count).transpose(2, 1, 0, 3)
+    summed = lax.psum_scatter(by_cycle, "ell", scatter_dimension=0, tiled=True)
+    owned = jnp.einsum(
+        "trkc,rksp->tspc",
+        summed,
+        psi_table(order_count, NPSI),
+        precision=lax.Precision.HIGHEST,
+    )
     return to_phi(
         lax.all_to_all(owned, "blk", split_axis=2, concat_axis=3, tiled=True), order_of_column
     )

time: 435 us -> 133 us (0.31)
  local copies, waits for them, and re-layouts: 187 us -> 8.39 us
  other arithmetic: 160 us -> 2.51 us
  Pallas kernels: 0 us -> 64 us
  matrix products: 36.2 us -> 9.25 us
    gather x1 -> x0, local copies, waits for them, and re-layouts: 121 us -> none  [on_device(): picked = jnp.take(beam_rows, slot_ell, axis=0)]
    another operation x2 -> x0, other arithmetic: 89.3 us -> none  [on_device(): jnp.stack([sky_alm[0] * beam_slots[0] - sky_alm[1] * beam_slots[1], sky_a...]
    pallas_call x0 -> x1, Pallas kernels: none -> 64 us  [order_sums(): pl.pallas_call(functools.partial(sums_kernel, orders, sub), out_shape=jax...]
    another operation x1 -> x0, local copies, waits for them, and re-layouts: 38.5 us -> none  [on_device(): jnp.stack([sky_alm[0] * beam_slots[0] - sky_alm[1] * beam_slots[1], sky_a...]
    select_n x2 -> x0, other arithmetic: 37.4 us -> none  [on_device(): picked = jnp.take(beam_rows, slot_ell, axis=0)]
    dot_general x1 -> x0, other arithmetic: 30.2 us -> none  [on_device(): jnp.dot(values.reshape(-1, slot_count), one_hot, preferred_element_type=j...]
    dot_general x2 -> x1, matrix products: 28.2 us -> 1.21 us  [on_device(): jnp.einsum('trkc,rksp->tspc', summed, psi_table(order_count, NPSI), preci...]
    convert_element_type x1 -> x0, local copies, waits for them, and re-layouts: 22 us -> none  [on_device(): wigner[:, None].astype(jnp.float32) * coeffs[None]]
  transfers between devices with their start and end apart: 2 -> 2, of which waited for: 2 -> 2; matrix products, arithmetic and copies ran while one was open for 1% -> 2% of each run, Pallas kernels for 0% -> 0%
where the time goes in v1:
time: 133 us; the launch traced here: 132 us
  Pallas kernels  64 us (48%)
  waiting for transfers between devices  29.8 us (22%)
  between operations  13.5 us (10%)
  matrix products  9.25 us (7%)
  local copies, waits for them, and re-layouts  8.39 us (6%)
  starting transfers between devices  4.61 us (3%)
  other arithmetic  2.51 us (2%)
    pallas_call x1, Pallas kernels, order_sums(): pl.pallas_call(functools.partial(sums_kernel, orders, sub), out_shape=jax...  64 us
    reduce_scatter x1, waiting for transfers between devices, on_device(): summed = lax.psum_scatter(by_cycle, 'ell', scatter_dimension=0, tiled=True)  25.5 us
    all_to_all x1, starting transfers between devices, on_device(): lax.all_to_all(owned, 'blk', split_axis=2, concat_axis=3, tiled=True)  4.6 us
    all_to_all x1, waiting for transfers between devices, on_device(): lax.all_to_all(owned, 'blk', split_axis=2, concat_axis=3, tiled=True)  4.25 us
    dot_general x1, matrix products, to_phi(): jnp.einsum('tpcj,cv->tpvj', weighted_im, select, precision=highest)  3.48 us
    dot_general x1, matrix products, to_phi(): jnp.einsum('tpcj,cv->tpvj', weighted_re, select, precision=highest)  3.47 us
  transfers between devices with their start and end apart: 2, of which 2 were waited for; matrix products, arithmetic and copies ran while one was open for 2% of the time, Pallas kernels for 0%

profile of v1, /device:TPU:0, one launch (start us, length us, event | category | flops | bytes accessed | tf_op | source)
XLA Modules:
  0.0 132.1 jit_solution(4371423480498607210)
XLA Ops:
  6.5 0.8 slice_bitcast_fusion.2
  7.3 1.3 %fusion.86 = (f32[1,16,2048]{2,0,1:T(1,128)S(1)}, f32[1,16,2048]{2,0,1:T(1,128)S(1)}) fusion(f32[2,17,2048]{2,0,1:T(2,128)} %param.8), kind=kLoop, calls=%fused_computation.115 | loop fusion | bytes 524288 | tf_op jit(solution)/shard_map/slice | solution.py:72
  8.8 1.1 broadcast_in_dim.4.col_ref
  9.9 1.1 broadcast_in_dim.5.ell_ref
  11.1 0.1 concatenate.19
  11.2 1.0 copy-done
  12.2 64.0 %order_sums.1 = f32[272,256]{1,0:T(8,128)S(1)} custom-call(bf16[17,8,65664]{2,1,0:T(8,128)(2,1)} %bitcast.75, f32[2,65664]{1,0:T(2,128)S(1)} %copy-done, s32[1,65664]{1,0:T(1,128)S(1)} %broadcast_in_dim.4.col_ref, s32[1,65664]{1,0:T(1,128)S(1)} %broadcast_in_dim.5.ell_ref, f32[16,40,128]{2,1,0:T(8,128)S(1)} %bitcast.73), custom_call_target="tpu_custom_call" | custom-call | tf_op jit(solution)/shard_map/order_sums/pallas_call | solution.py:210
  76.3 0.9 copy.39
  77.4 25.5 %reduce-scatter.2.cloned.1.call-done = f32[2,2,17,256]{3,2,1,0:T(8,128)} async-done(((f32[8,2,17,256]{3,2,1,0:T(8,128)}), f32[2,2,17,256]{3,2,1,0:T(8,128)}) %reduce-scatter.2.cloned.1.call-update) | async-done | bytes 69648 | tf_op jit(solution)/shard_map/reduce_scatter | solution.py:241
  102.9 1.2 convolution_bitcast_fusion
  104.2 0.8 copy.28
  104.9 4.6 %all-to-all-start = ((f32[2,2,32,256]{3,0,1,2:T(2,128)}), f32[2,2,32,256]{3,0,1,2:T(2,128)S(1)}, u32[]{:S(2)}, u32[]{:S(2)}) async-start(f32[2,2,32,256]{3,0,1,2:T(2,128)} %copy.28), calls=%async_computation.1 | async-start | bytes 262144 | tf_op jit(solution)/shard_map/all_to_all | solution.py:249
  109.5 2.0 %fusion.36 = (f32[2048,64]{0,1:T(8,128)S(1)}, f32[2048,64]{0,1:T(8,128)S(1)}) fusion(s32[2048]{0:T(1024)S(1)} %get-tuple-element.14), kind=kLoop, calls=%fused_computation.41 | loop fusion | flops 1835008 | bytes 1056768 | tf_op jit(solution)/shard_map/cos | solution.py:45
  111.6 0.1 fusion.63
  111.7 0.1 copy.30
  111.8 0.2 fusion.62
  111.9 0.1 copy.31
  112.0 4.3 %all-to-all-done = f32[2,2,32,256]{3,0,1,2:T(2,128)S(1)} async-done(((f32[2,2,32,256]{3,0,1,2:T(2,128)}), f32[2,2,32,256]{3,0,1,2:T(2,128)S(1)}, u32[]{:S(2)}, u32[]{:S(2)}) %all-to-all-start) | async-done | bytes 131104 | tf_op jit(solution)/shard_map/all_to_all | solution.py:249
  116.3 0.1 copy.40
  116.4 3.5 %fusion.4 = f32[64,2,4,64]{3,0,2,1:T(8,128)S(1)} fusion(f32[2048,64]{0,1:T(8,128)S(1)} %get-tuple-element.16, f32[2,4,2048]{2,1,0:T(4,128)S(1)} %get-tuple-element.10, f32[2048,64]{0,1:T(8,128)S(1)} %get-tuple-element.15, f32[2,4,2048]{2,1,0:T(4,128)S(1)} %get-tuple-element.9, s32[2048]{0:T(1024)S(1)} %get-tuple-element.13), kind=kOutput, calls=%fused_computation.4 | convolution fusion | flops 808583168 | bytes 1318912 | tf_op jit(solution)/shard_map/tpcj,cv->tpvj/dot_general | solution.py:52
  119.9 3.5 %fusion = f32[64,2,4,64]{3,0,2,1:T(8,128)S(1)} fusion(f32[2048,64]{0,1:T(8,128)S(1)} %get-tuple-element.16, f32[2,4,2048]{2,1,0:T(4,128)S(1)} %get-tuple-element.10, f32[2048,64]{0,1:T(8,128)S(1)} %get-tuple-element.15, f32[2,4,2048]{2,1,0:T(4,128)S(1)} %get-tuple-element.9, s32[2048]{0:T(1024)S(1)} %get-tuple-element.13), kind=kOutput, calls=%fused_computation | convolution fusion | flops 808583168 | bytes 1318912 | tf_op jit(solution)/shard_map/tpcj,cv->tpvj/dot_general | solution.py:53
  123.4 0.5 fusion.27
  123.9 0.5 fusion.16
  124.5 0.8 reshape.177
  (14 shorter events, 0.4 us)
Async XLA Ops:
  6.5 96.4 %reduce-scatter.2.cloned.1.call-start = ((), (), s32[]{:S(2)}) async-start(), calls=%async_computation.2 | async-start | bytes 491520 | tf_op jit(solution)/shard_map/reduce_scatter | solution.py:241
  11.2 1.0 copy-start
  12.2 65.1 %copy-start.1 = (s32[2048]{0:T(1024)S(1)}, s32[2048]{0:T(1024)}, u32[]{:S(2)}) copy-start(s32[2048]{0:T(1024)} %param.11) | copy-start | bytes 24580
  104.9 11.4 %all-to-all-start = ((f32[2,2,32,256]{3,0,1,2:T(2,128)}), f32[2,2,32,256]{3,0,1,2:T(2,128)S(1)}, u32[]{:S(2)}, u32[]{:S(2)}) async-start(f32[2,2,32,256]{3,0,1,2:T(2,128)} %copy.28), calls=%async_computation.1 | async-start | bytes 262144 | tf_op jit(solution)/shard_map/all_to_all | solution.py:249
Sparse Core Ops, SparseCore 0:
  77.3 25.5 reduce-scatter.1

commit v2 on v1

--- a/solution.py
+++ b/solution.py
@@ -37,7 +37,7 @@
     period = 2 * degrees
     inner = 2 ** ((period.bit_length() - 1) // 2)
     outer = period // inner
-    highest = lax.Precision.HIGHEST
+    highest = lax.Precision.HIGH
     high_part = order_of_column // inner
     low_part = order_of_column % inner
     turns = high_part[:, None] * jnp.arange(outer, dtype=jnp.int32)[None, :] % outer
@@ -98,7 +98,7 @@
 
 
 def sums_kernel(
-    orders, sub, wig_ref, sky_ref, col_ref, ell_ref, table_ref, out_ref, coeff_ref, value_ref, hot_ref
+    orders, sub, wig_ref, sky_ref, col_ref, ell_ref, table_ref, out_ref, *scratch
 ):
     cycles = wig_ref.shape[1]
     chunk = wig_ref.shape[2]
@@ -107,7 +107,8 @@
     whole = orders // SUBLANES
     rest = orders - whole * SUBLANES
     packed = 0 < rest <= SUBLANES // 4
-    cols = hot_ref.shape[0]
+    coeff_refs, value_refs, hot_refs = scratch[0:2], scratch[2:4], scratch[4:6]
+    cols = out_ref.shape[1]
     parts = sub // LANES
 
     live = col_ref[...] >= 0
@@ -116,7 +117,7 @@
     low = jnp.min(jnp.where(live, degree, tiles * LANES - 1).astype(jnp.float32)).astype(jnp.int32) // LANES
     span = top - low + 1
 
-    def pick_all(count, first, start):
+    def pick_all(count, first, start, coeff_ref):
         for part in range(parts):
             lanes = pl.ds(pl.multiple_of(start + part * LANES, LANES), LANES)
             ell = jnp.broadcast_to(ell_ref[:, lanes], (SUBLANES, LANES))
@@ -153,22 +154,50 @@
         return 2 * whole * SUBLANES + part * step + order - whole * SUBLANES
 
     def run(count, first):
-        @pl.loop(0, chunk // sub)
-        def _(step):
-            start = pl.multiple_of(step * sub, LANES)
-            pick_all(count, first, start)
+        halves = chunk // sub
+
+        def products(half, which):
+            start = pl.multiple_of(half * sub, LANES)
+            coeff, value, hot = coeff_refs[which], value_refs[which], hot_refs[which]
+            pick_all(count, first, start, coeff)
             lanes = pl.ds(start, sub)
             for order in range(orders):
                 wig = wig_ref[order, :, lanes].astype(jnp.float32)
-                real = wig * coeff_ref[pl.ds(row_of(0, order), 1), :]
-                imag = wig * coeff_ref[pl.ds(row_of(1, order), 1), :]
+                real = wig * coeff[pl.ds(row_of(0, order), 1), :]
+                imag = wig * coeff[pl.ds(row_of(1, order), 1), :]
                 both = jnp.concatenate([real, imag], axis=0).astype(jnp.bfloat16)
-                value_ref[pl.ds(order * 2 * cycles, 2 * cycles), lanes] = both
+                value[pl.ds(order * 2 * cycles, 2 * cycles), :] = both
             col = jnp.broadcast_to(col_ref[:, lanes], (cols, sub))
             row = lax.broadcasted_iota(jnp.int32, (cols, sub), 0)
-            hot_ref[:, lanes] = (row == col).astype(jnp.float32).astype(jnp.bfloat16)
-
-    counts = sorted({min(c, tiles) for c in (4, 5, 9)})
+            hot[...] = (row == col).astype(jnp.float32).astype(jnp.bfloat16)
+
+        def add_up(which):
+            out_ref[...] += lax.dot_general(
+                value_refs[which][...],
+                hot_refs[which][...],
+                (((1,), (1,)), ((), ())),
+                preferred_element_type=jnp.float32,
+            )
+
+        products(0, 1)
+
+        @pl.loop(0, (halves - 1) // 2)
+        def _(pair):
+            add_up(1)
+            products(2 * pair + 1, 0)
+            add_up(0)
+            products(2 * pair + 2, 1)
+
+        add_up(1)
+        if halves % 2 == 0:
+            products(halves - 1, 0)
+            add_up(0)
+
+    @pl.when(pl.program_id(0) == 0)
+    def _():
+        out_ref[...] = jnp.zeros_like(out_ref)
+
+    counts = sorted({min(c, tiles) for c in (4, 9)})
     below = 0
     for count in counts:
         first = jnp.minimum(low, tiles - count)
@@ -183,21 +212,6 @@
         @pl.when(span > below)
         def _():
             run(tiles, 0)
-
-    part = lax.dot_general(
-        value_ref[...],
-        hot_ref[...],
-        (((1,), (1,)), ((), ())),
-        preferred_element_type=jnp.float32,
-    )
-
-    @pl.when(pl.program_id(0) == 0)
-    def _():
-        out_ref[...] = part
-
-    @pl.when(pl.program_id(0) > 0)
-    def _():
-        out_ref[...] += part
 
 
 def order_sums(wigner, sky_alm, beam_blm, slot_col, slot_ell, cols):
@@ -220,9 +234,9 @@
         ],
         out_specs=pl.BlockSpec((rows, cols), lambda i: (0, 0)),
         scratch_shapes=[
-            pltpu.VMEM((table.shape[1], sub), jnp.float32),
-            pltpu.VMEM((rows, chunk), jnp.bfloat16),
-            pltpu.VMEM((cols, chunk), jnp.bfloat16),
+            *[pltpu.VMEM((table.shape[1], sub), jnp.float32) for _ in range(2)],
+            *[pltpu.VMEM((rows, sub), jnp.bfloat16) for _ in range(2)],
+            *[pltpu.VMEM((cols, sub), jnp.bfloat16) for _ in range(2)],
         ],
         compiler_params=pltpu.CompilerParams(
             dimension_semantics=("arbitrary",), vmem_limit_bytes=48 * 1024 * 1024
@@ -238,7 +252,9 @@
     col_count = order_of_column.shape[0] // blk_count
     col_sums = order_sums(wigner, sky_alm, beam_blm, slot_col, slot_ell, col_count)
     by_cycle = col_sums.reshape(order_count, 2, cycle_total, col_count).transpose(2, 1, 0, 3)
-    summed = lax.psum_scatter(by_cycle, "ell", scatter_dimension=0, tiled=True)
+    ell_count = lax.axis_size("ell")
+    partials = by_cycle.reshape((ell_count, cycle_total // ell_count) + by_cycle.shape[1:])
+    summed = lax.all_to_all(partials, "ell", split_axis=0, concat_axis=0, tiled=True).sum(axis=0)
     owned = jnp.einsum(
         "trkc,rksp->tspc",
         summed,

time: 133 us -> 84.7 us (0.64)
  waiting for transfers between devices: 29.8 us -> 9.48 us
  Pallas kernels: 64 us -> 47.7 us
  between operations: 13.5 us -> 0.16 us
  starting transfers between devices: 4.61 us -> 10.1 us
  matrix products: 9.25 us -> 5.46 us
    reduce_scatter x1 -> x0, waiting for transfers between devices: 25.5 us -> none  [on_device(): summed = lax.psum_scatter(by_cycle, 'ell', scatter_dimension=0, tiled=True)]
    pallas_call x1, Pallas kernels: 64 us -> 47.7 us  [order_sums(): pl.pallas_call(functools.partial(sums_kernel, orders, sub), out_shape=jax...]
    all_to_all x0 -> x1, waiting for transfers between devices: none -> 5.23 us  [on_device(): lax.all_to_all(partials, 'ell', split_axis=0, concat_axis=0, tiled=True)]
    all_to_all x0 -> x1, starting transfers between devices: none -> 4.89 us  [on_device(): lax.all_to_all(partials, 'ell', split_axis=0, concat_axis=0, tiled=True)]
    dot_general x1, matrix products: 3.48 us -> 2.14 us  [to_phi(): jnp.einsum('tpcj,cv->tpvj', weighted_im, select, precision=highest)]
    dot_general x1, matrix products: 3.47 us -> 2.14 us  [to_phi(): jnp.einsum('tpcj,cv->tpvj', weighted_re, select, precision=highest)]
  transfers between devices with their start and end apart: 2 -> 2, of which waited for: 2 -> 2; matrix products, arithmetic and copies ran while one was open for 2% -> 3% of each run, Pallas kernels for 0% -> 0%
where the time goes in v2:
time: 84.7 us; the launch traced here: 84.1 us
  Pallas kernels  47.7 us (56%)
  starting transfers between devices  10.1 us (12%)
  waiting for transfers between devices  9.48 us (11%)
  local copies, waits for them, and re-layouts  8.47 us (10%)
  matrix products  5.46 us (6%)
  other arithmetic  2.63 us (3%)
    pallas_call x1, Pallas kernels, order_sums(): pl.pallas_call(functools.partial(sums_kernel, orders, sub), out_shape=jax...  47.7 us
    all_to_all x1, starting transfers between devices, on_device(): lax.all_to_all(owned, 'blk', split_axis=2, concat_axis=3, tiled=True)  5.25 us
    all_to_all x1, waiting for transfers between devices, on_device(): lax.all_to_all(partials, 'ell', split_axis=0, concat_axis=0, tiled=True)  5.23 us
    all_to_all x1, starting transfers between devices, on_device(): lax.all_to_all(partials, 'ell', split_axis=0, concat_axis=0, tiled=True)  4.89 us
    all_to_all x1, waiting for transfers between devices, on_device(): lax.all_to_all(owned, 'blk', split_axis=2, concat_axis=3, tiled=True)  4.25 us
    dot_general x1, matrix products, to_phi(): jnp.einsum('tpcj,cv->tpvj', weighted_im, select, precision=highest)  2.14 us
    dot_general x1, matrix products, to_phi(): jnp.einsum('tpcj,cv->tpvj', weighted_re, select, precision=highest)  2.14 us
    cos x1, other arithmetic, to_phi(): cos_first = jnp.cos(angle)  2.04 us
  transfers between devices with their start and end apart: 2, of which 2 were waited for; matrix products, arithmetic and copies ran while one was open for 3% of the time, Pallas kernels for 0%

profile of v2, /device:TPU:0, one launch (start us, length us, event | category | flops | bytes accessed | tf_op | source)
XLA Modules:
  0.0 84.1 jit_solution(12360023628827284778)
XLA Ops:
  0.0 0.8 slice_bitcast_fusion.2
  0.8 1.3 %fusion.87 = (f32[1,16,2048]{2,0,1:T(1,128)S(1)}, f32[1,16,2048]{2,0,1:T(1,128)S(1)}) fusion(f32[2,17,2048]{2,0,1:T(2,128)} %param.8), kind=kLoop, calls=%fused_computation.115 | loop fusion | bytes 524288 | tf_op jit(solution)/shard_map/slice | solution.py:72
  2.3 1.1 %broadcast_in_dim.4.col_ref = s32[1,65664]{1,0:T(1,128)S(1)} reshape(s32[65664]{0:T(1024)} %param.9) | data formatting | bytes 525312 | tf_op jit(solution)/shard_map/broadcast_in_dim | solution.py:245
  3.4 1.1 %broadcast_in_dim.5.ell_ref = s32[1,65664]{1,0:T(1,128)S(1)} reshape(s32[65664]{0:T(1024)} %param.10) | data formatting | bytes 525312 | tf_op jit(solution)/shard_map/broadcast_in_dim | solution.py:245
  4.7 1.0 %copy-done = f32[2,65664]{1,0:T(2,128)S(1)} copy-done((f32[2,65664]{1,0:T(2,128)S(1)}, f32[2,65664]{1,0:T(2,128)}, u32[]{:S(2)}) %copy-start) | copy-done | bytes 525336
  5.7 47.7 %order_sums.1 = f32[272,256]{1,0:T(8,128)S(1)} custom-call(bf16[17,8,65664]{2,1,0:T(8,128)(2,1)} %bitcast.75, f32[2,65664]{1,0:T(2,128)S(1)} %copy-done, s32[1,65664]{1,0:T(1,128)S(1)} %broadcast_in_dim.4.col_ref, s32[1,65664]{1,0:T(1,128)S(1)} %broadcast_in_dim.5.ell_ref, f32[16,40,128]{2,1,0:T(8,128)S(1)} %bitcast.73), custom_call_target="tpu_custom_call" | custom-call | tf_op jit(solution)/shard_map/order_sums/pallas_call | solution.py:224
  53.4 0.1 copy.26
  53.6 0.9 %copy.27 = f32[4,2,2,17,256]{4,1,2,3,0:T(2,128)} copy(f32[4,2,2,17,256]{4,2,3,1,0:T(2,128)S(1)} %bitcast.76) | data formatting | bytes 557056 | tf_op jit(solution)/shard_map/reshape | solution.py:256
  54.4 4.9 %all-to-all-start = ((f32[4,2,2,17,256]{4,1,2,3,0:T(2,128)}), f32[4,2,2,17,256]{4,1,2,3,0:T(2,128)S(1)}, u32[]{:S(2)}, u32[]{:S(2)}) async-start(f32[4,2,2,17,256]{4,1,2,3,0:T(2,128)} %copy.27), calls=%async_computation | async-start | bytes 557056 | tf_op jit(solution)/shard_map/all_to_all | solution.py:257
  59.5 5.2 %all-to-all-done = f32[4,2,2,17,256]{4,1,2,3,0:T(2,128)S(1)} async-done(((f32[4,2,2,17,256]{4,1,2,3,0:T(2,128)}), f32[4,2,2,17,256]{4,1,2,3,0:T(2,128)S(1)}, u32[]{:S(2)}, u32[]{:S(2)}) %all-to-all-start) | async-done | bytes 278560 | tf_op jit(solution)/shard_map/all_to_all | solution.py:257
  64.7 0.1 reduce_sum.9
  64.9 0.3 convolution_bitcast_fusion
  65.2 0.8 copy.30
  65.9 5.2 %all-to-all-start.1 = ((f32[2,2,32,256]{3,0,1,2:T(2,128)}), f32[2,2,32,256]{3,0,1,2:T(2,128)S(1)}, u32[]{:S(2)}, u32[]{:S(2)}) async-start(f32[2,2,32,256]{3,0,1,2:T(2,128)} %copy.30), calls=%async_computation.1 | async-start | bytes 262144 | tf_op jit(solution)/shard_map/all_to_all | solution.py:265
  71.2 2.0 %fusion.36 = (f32[2048,64]{0,1:T(8,128)S(1)}, f32[2048,64]{0,1:T(8,128)S(1)}) fusion(s32[2048]{0:T(1024)S(1)} %get-tuple-element.14), kind=kLoop, calls=%fused_computation.40 | loop fusion | flops 1835008 | bytes 1056768 | tf_op jit(solution)/shard_map/cos | solution.py:45
  73.2 0.1 fusion.64
  73.5 0.2 fusion.63
  73.7 4.3 %all-to-all-done.1 = f32[2,2,32,256]{3,0,1,2:T(2,128)S(1)} async-done(((f32[2,2,32,256]{3,0,1,2:T(2,128)}), f32[2,2,32,256]{3,0,1,2:T(2,128)S(1)}, u32[]{:S(2)}, u32[]{:S(2)}) %all-to-all-start.1) | async-done | bytes 131104 | tf_op jit(solution)/shard_map/all_to_all | solution.py:265
  77.9 0.1 copy.45
  78.1 2.1 %fusion.4 = f32[64,2,4,64]{3,0,2,1:T(8,128)S(1)} fusion(f32[2048,64]{0,1:T(8,128)S(1)} %get-tuple-element.16, f32[2,4,2048]{2,1,0:T(4,128)S(1)} %get-tuple-element.10, f32[2048,64]{0,1:T(8,128)S(1)} %get-tuple-element.15, f32[2,4,2048]{2,1,0:T(4,128)S(1)} %get-tuple-element.9, s32[2048]{0:T(1024)S(1)} %get-tuple-element.13), kind=kOutput, calls=%fused_computation.4 | convolution fusion | flops 405929984 | bytes 1318912 | tf_op jit(solution)/shard_map/tpcj,cv->tpvj/dot_general | solution.py:52
  80.3 2.1 %fusion = f32[64,2,4,64]{3,0,2,1:T(8,128)S(1)} fusion(f32[2048,64]{0,1:T(8,128)S(1)} %get-tuple-element.16, f32[2,4,2048]{2,1,0:T(4,128)S(1)} %get-tuple-element.10, f32[2048,64]{0,1:T(8,128)S(1)} %get-tuple-element.15, f32[2,4,2048]{2,1,0:T(4,128)S(1)} %get-tuple-element.9, s32[2048]{0:T(1024)S(1)} %get-tuple-element.13), kind=kOutput, calls=%fused_computation | convolution fusion | flops 405929984 | bytes 1318912 | tf_op jit(solution)/shard_map/tpcj,cv->tpvj/dot_general | solution.py:53
  82.4 0.4 fusion.27
  82.8 0.4 fusion.16
  83.3 0.8 reshape.181
  (15 shorter events, 0.6 us)
Async XLA Ops:
  4.6 1.0 %copy-start = (f32[2,65664]{1,0:T(2,128)S(1)}, f32[2,65664]{1,0:T(2,128)}, u32[]{:S(2)}) copy-start(f32[2,65664]{1,0:T(2,128)} %sky_ref.1) | copy-start | bytes 1575940
  5.7 53.8 %copy-start.1 = (s32[2048]{0:T(1024)S(1)}, s32[2048]{0:T(1024)}, u32[]{:S(2)}) copy-start(s32[2048]{0:T(1024)} %param.11) | copy-start | bytes 24580
  54.4 10.3 %all-to-all-start = ((f32[4,2,2,17,256]{4,1,2,3,0:T(2,128)}), f32[4,2,2,17,256]{4,1,2,3,0:T(2,128)S(1)}, u32[]{:S(2)}, u32[]{:S(2)}) async-start(f32[4,2,2,17,256]{4,1,2,3,0:T(2,128)} %copy.27), calls=%async_computation | async-start | bytes 557056 | tf_op jit(solution)/shard_map/all_to_all | solution.py:257
  65.9 12.0 %all-to-all-start.1 = ((f32[2,2,32,256]{3,0,1,2:T(2,128)}), f32[2,2,32,256]{3,0,1,2:T(2,128)S(1)}, u32[]{:S(2)}, u32[]{:S(2)}) async-start(f32[2,2,32,256]{3,0,1,2:T(2,128)} %copy.30), calls=%async_computation.1 | async-start | bytes 262144 | tf_op jit(solution)/shard_map/all_to_all | solution.py:265
